TPU v7x, 32 devices: a whole 2x2x4 slice. The times are simulated.
32 devices in a mesh: pts: 8 (over y, x, core), cand: 4 (over z).
Axes of the slice: x: 2, y: 2, z: 4, core: 2. Of those that a mesh axis runs over, the one named last changes fastest.
Arguments:
- points: bfloat16 [8192, 1024], P('pts'), may hold values from -6 to 6
- weights: float32 [8192], P('pts'), may hold values from 0.5 to 5
- coverage: float32 [8192], P('pts'), may hold values from -0.5 to 1
- candidates: bfloat16 [4096, 1024], P('cand'), may hold values from -6 to 6
- picks: int32 [64], replicated, may hold values from 0 to 4095
Outputs:
- gains: float32 [4096], P('cand')
- top_gains: float32 [64], replicated
- new_coverage: float32 [8192], P('pts')
All inputs are finite; a program needn't handle non-finite values.
Results may differ from a plain program's by a relative error of at most 0.0003.
Values may be sent and summed in bfloat16 or wider, within the bound.
A program may use at most 64 MiB of HBM per device.

v0:
```python
import jax
import jax.numpy as jnp
from jax import lax
from jax.sharding import PartitionSpec as P

TOPK = 64


def joined(x, axis, combine):
    everything = lax.all_gather(x, axis)
    leading = everything[0]

    def hop(k, so_far):
        return combine(so_far, everything[k])

    return lax.fori_loop(1, lax.axis_size(axis), hop, leading)


def best_values(first, second):
    return lax.top_k(jnp.concatenate([first, second]), TOPK)[0]


def on_device(points, weights, coverage, candidates, picks):
    scale = points.shape[1] ** (-0.5)
    total = points.shape[0] * lax.axis_size("pts")
    cand_rows = candidates.shape[0]
    offset = lax.axis_index("cand") * cand_rows
    sims = jnp.dot(points, candidates.T, preferred_element_type=jnp.float32) * scale
    partial_value = (
        jnp.sum(weights[:, None] * jnp.maximum(sims - coverage[:, None], 0.0), axis=0) / total
    )
    gains = lax.psum(partial_value, "pts")
    top_gains = joined(lax.top_k(gains, TOPK)[0], "cand", best_values)
    columns = offset + jnp.arange(cand_rows, dtype=jnp.int32)
    chosen = jnp.any(picks[:, None] == columns[None, :], axis=0)
    local_best = jnp.max(jnp.where(chosen[None, :], sims, -1e30), axis=1)
    best_sim = lax.pmax(local_best, "cand")
    new_coverage = jnp.maximum(coverage, best_sim)
    return (gains, top_gains, new_coverage)


def solution(mesh):
    placed = (P("pts", None), P("pts"), P("pts"), P("cand", None), P())
    return jax.shard_map(
        on_device, mesh=mesh, in_specs=placed, out_specs=(P("cand"), P(), P("pts")), check_vma=False
    )
```

profile of v0, /device:TPU:0, one launch (start us, length us, event | category | flops | bytes accessed | tf_op | source)
XLA Modules:
  0.0 56.5 jit_solution(17969848759909569890)
XLA Ops:
  0.6 0.0 copy-start
  0.7 0.9 %compare_reduce_fusion = pred[1024]{0:T(1024)(128)(4,1)S(1)} fusion(s32[1024]{0:T(1024)S(1)} %iota_add_fusion, s32[64]{0:T(128)} %param.11), kind=kLoop, calls=%fused_computation.4 | loop fusion | flops 130048 | bytes 5376 | tf_op jit(solution)/shard_map/reduce_or | solution.py:35
  1.6 0.7 %copy-done = bf16[1024,1024]{1,0:T(8,128)(2,1)S(1)} copy-done((bf16[1024,1024]{1,0:T(8,128)(2,1)S(1)}, bf16[1024,1024]{1,0:T(8,128)(2,1)}, u32[]{:S(2)}) %copy-start) | copy-done | bytes 2097176
  2.2 0.0 copy-start.3
  2.2 4.4 %select_reduce_fusion = (f32[1024]{0:T(1024)S(1)}, f32[1024]{0:T(1024)S(1)}) fusion(pred[1024]{0:T(1024)(128)(4,1)S(1)} %compare_reduce_fusion, f32[1024]{0:T(1024)} %param.9, f32[1024]{0:T(1024)} %param.8, bf16[1024,1024]{1,0:T(8,128)(2,1)S(1)} %copy-done, bf16[1024,1024]{1,0:T(8,128)(2,1)} %param.10), kind=kOutput, calls=%fused_computation.2 | convolution fusion | flops 2154821632 | bytes 4211712 | tf_op jit(solution)/shard_map/dot_general | solution.py:28
  6.6 15.2 %psum.7 = f32[1024]{0:T(1024)S(1)} all-reduce(f32[1024]{0:T(1024)S(1)} %broadcast_multiply_fusion), channel_id=1, replica_groups=mesh['pts'=8,'cand'=4] {'pts'}, use_global_device_ids=true, to_apply=%region_1.0 | all-reduce | flops 1024 | bytes 8192 | tf_op jit(solution)/shard_map/psum | solution.py:32
  21.8 4.4 %top_k.14 = (f32[1024]{0:T(1024)S(1)}, s32[1024]{0:T(1024)}) sort(f32[1024]{0:T(1024)S(1)} %psum.7, s32[1024]{0:T(1024)S(1)} %iota.11), dimensions={0}, to_apply=%region_2.0 | sort | flops 10240 | bytes 16384 | tf_op jit(solution)/shard_map/top_k | solution.py:33
  26.2 0.0 copy-done.3
  26.2 0.6 %dynamic-slice = u32[1]{0:T(128)} dynamic-slice(u32[32]{0:T(128)S(1)} %copy-done.3, u32[]{:T(128)S(6)} %add.47), dynamic_slice_sizes={1} | dynamic-slice | bytes 12
  27.5 0.1 slice_dynamic-update-slice_fusion
  27.6 11.9 %all-reduce = f32[256]{0:T(256)S(1)} all-reduce(f32[256]{0:T(256)S(1)} %slice_dynamic-update-slice_fusion), channel_id=2, replica_groups=mesh['pts'=8,'cand'=4] {'cand'}, use_global_device_ids=true, to_apply=%add | all-reduce | flops 256 | bytes 2048
  39.5 0.1 reshape.14
  39.6 8.0 %while.15 = (s32[]{:T(128)}, f32[64]{0:T(128)S(1)}, f32[4,64]{1,0:T(4,128)S(1)}, s32[]{:T(128)}, s32[]{:T(128)}, /*index=5*/s32[]{:T(128)}) while((s32[]{:T(128)}, f32[64]{0:T(128)S(1)}, f32[4,64]{1,0:T(4,128)S(1)}, s32[]{:T(128)}, s32[]{:T(128)}, /*index=5*/s32[]{:T(128)}) %tuple.41), condition=%wide.region_5.6_spmd, body=%wide.region_3.5_spmd.sunk | while | flops 1029 | bytes 4211 | solution.py:16
  39.6 0.1 pad_maximum_fusion.2
  39.7 2.6 %top_k.22 = (f32[128]{0:T(128)S(1)}, s32[128]{0:T(128)}) sort(f32[128]{0:T(128)S(1)} %pad_maximum_fusion.2, s32[128]{0:T(128)S(1)} %iota.15), dimensions={0}, to_apply=%region_4.4 | sort | flops 896 | bytes 2048 | tf_op jit(solution)/shard_map/while/body/eval_jaxpr/top_k | solution.py:20
  42.2 0.1 pad_maximum_fusion.2
  42.3 2.6 %top_k.22 = (f32[128]{0:T(128)S(1)}, s32[128]{0:T(128)}) sort(f32[128]{0:T(128)S(1)} %pad_maximum_fusion.2, s32[128]{0:T(128)S(1)} %iota.15), dimensions={0}, to_apply=%region_4.4 | sort | flops 896 | bytes 2048 | tf_op jit(solution)/shard_map/while/body/eval_jaxpr/top_k | solution.py:20
  44.9 0.1 pad_maximum_fusion.2
  45.0 2.6 %top_k.22 = (f32[128]{0:T(128)S(1)}, s32[128]{0:T(128)}) sort(f32[128]{0:T(128)S(1)} %pad_maximum_fusion.2, s32[128]{0:T(128)S(1)} %iota.15), dimensions={0}, to_apply=%region_4.4 | sort | flops 896 | bytes 2048 | tf_op jit(solution)/shard_map/while/body/eval_jaxpr/top_k | solution.py:20
  47.5 8.3 %pmax.7 = f32[1024]{0:T(1024)S(1)} all-reduce(f32[1024]{0:T(1024)S(1)} %get-tuple-element.97), channel_id=1, replica_groups=mesh['pts'=8,'cand'=4] {'cand'}, use_global_device_ids=true, to_apply=%region_8.9 | all-reduce | flops 1024 | bytes 8192 | tf_op jit(solution)/shard_map/pmax | solution.py:37
  55.9 0.0 copy-done.2
  55.9 0.6 %max.13 = f32[1024]{0:T(1024)} maximum(f32[1024]{0:T(1024)S(1)} %copy-done.2, f32[1024]{0:T(1024)S(1)} %pmax.7) | non-fusion elementwise | flops 1024 | bytes 12288 | tf_op jit(solution)/shard_map/max | solution.py:38
  56.5 0.0 copy-done.1
  56.5 0.0 copy-done.4
  (14 shorter events, 0.0 us)
Async XLA Ops:
  0.6 1.6 %copy-start = (bf16[1024,1024]{1,0:T(8,128)(2,1)S(1)}, bf16[1024,1024]{1,0:T(8,128)(2,1)}, u32[]{:S(2)}) copy-start(bf16[1024,1024]{1,0:T(8,128)(2,1)} %param.7) | copy-start | bytes 6291460
  2.2 24.0 %copy-start.3 = (u32[32]{0:T(128)S(1)}, u32[32]{0:T(128)}, u32[]{:S(2)}) copy-start(u32[32]{0:T(128)} %constant.74) | copy-start | bytes 388
  2.2 53.6 %copy-start.2 = (f32[1024]{0:T(1024)S(1)}, f32[1024]{0:T(1024)}, u32[]{:S(2)}) copy-start(f32[1024]{0:T(1024)} %param.9) | copy-start | bytes 12292
  21.8 34.7 %copy-start.1 = (f32[1024]{0:T(1024)}, f32[1024]{0:T(1024)S(1)}, u32[]{:S(2)}) copy-start(f32[1024]{0:T(1024)S(1)} %psum.7) | copy-start | bytes 12292
  47.5 8.9 %copy-start.4 = (f32[64]{0:T(128)}, f32[64]{0:T(128)S(1)}, u32[]{:S(2)}) copy-start(f32[64]{0:T(128)S(1)} %get-tuple-element.93) | copy-start | bytes 772
where the time goes:
time: 56.7 us; the launch traced here: 56.5 us
  blocking collectives  35.4 us (62%)
  other arithmetic  13.9 us (25%)
  matrix products  4.37 us (8%)
  local copies, waits for them, and re-layouts  1.48 us (3%)
  between operations  1.34 us (2%)
    psum x1, blocking collectives, on_device(): gains = lax.psum(partial_value, 'pts')  15.2 us
    unnamed x1, blocking collectives  11.9 us
    pmax x1, blocking collectives, on_device(): best_sim = lax.pmax(local_best, 'cand')  8.34 us
    top_k x3, other arithmetic, best_values(): return lax.top_k(jnp.concatenate([first, second]), TOPK)[0]  7.7 us
    top_k x1, other arithmetic, on_device(): top_gains = joined(lax.top_k(gains, TOPK)[0], 'cand', best_values)  4.43 us
    dot_general x1, matrix products, on_device(): jnp.dot(points, candidates.T, preferred_element_type=jnp.float32) * scale  4.37 us
    unnamed x13, local copies, waits for them, and re-layouts  1.37 us

commit v1 on v0

--- a/solution.py
+++ b/solution.py
@@ -4,6 +4,14 @@
 from jax.sharding import PartitionSpec as P
 
 TOPK = 64
+
+
+def doubling_sum(x, name):
+    size, total = (lax.axis_size(name), x)
+    for far in [1 << k for k in range(size.bit_length() - 1)]:
+        pairs = [(i, i ^ far) for i in range(size)]
+        total = total + lax.ppermute(total, name, pairs)
+    return total
 
 
 def joined(x, axis, combine):
@@ -29,7 +37,7 @@
     partial_value = (
         jnp.sum(weights[:, None] * jnp.maximum(sims - coverage[:, None], 0.0), axis=0) / total
     )
-    gains = lax.psum(partial_value, "pts")
+    gains = doubling_sum(partial_value, "pts")
     top_gains = joined(lax.top_k(gains, TOPK)[0], "cand", best_values)
     columns = offset + jnp.arange(cand_rows, dtype=jnp.int32)
     chosen = jnp.any(picks[:, None] == columns[None, :], axis=0)

time: 56.7 us -> 49.9 us (0.88)
  blocking collectives: 35.4 us -> 20.3 us
  starting transfers between devices: 0 us -> 5.43 us
  waiting for transfers between devices: 0 us -> 2.41 us
    psum x1 -> x0, blocking collectives: 15.2 us -> none  [on_device(): gains = lax.psum(partial_value, 'pts')]
    ppermute x0 -> x3, starting transfers between devices: none -> 5.43 us  [doubling_sum(): total = total + lax.ppermute(total, name, pairs)]
    unnamed x1, blocking collectives: 11.9 us -> 8.34 us
    pmax x1, blocking collectives: 8.34 us -> 11.9 us  [on_device(): best_sim = lax.pmax(local_best, 'cand')]
    ppermute x0 -> x3, waiting for transfers between devices: none -> 2.41 us  [doubling_sum(): total = total + lax.ppermute(total, name, pairs)]
  transfers between devices with their start and end apart: 0 -> 3, of which waited for: 0 -> 2; matrix products, arithmetic and copies ran while one was open for 0% -> 2% of each run, Pallas kernels for 0% -> 0%
where the time goes in v1:
time: 49.9 us; the launch traced here: 49.7 us
  blocking collectives  20.3 us (41%)
  other arithmetic  13.9 us (28%)
  starting transfers between devices  5.43 us (11%)
  matrix products  4.37 us (9%)
  waiting for transfers between devices  2.41 us (5%)
  local copies, waits for them, and re-layouts  1.98 us (4%)
  between operations  1.35 us (3%)
    pmax x1, blocking collectives, on_device(): best_sim = lax.pmax(local_best, 'cand')  11.9 us
    unnamed x1, blocking collectives  8.34 us
    top_k x3, other arithmetic, best_values(): return lax.top_k(jnp.concatenate([first, second]), TOPK)[0]  7.7 us
    ppermute x3, starting transfers between devices, doubling_sum(): total = total + lax.ppermute(total, name, pairs)  5.43 us
    top_k x1, other arithmetic, on_device(): top_gains = joined(lax.top_k(gains, TOPK)[0], 'cand', best_values)  4.43 us
    dot_general x1, matrix products, on_device(): jnp.dot(points, candidates.T, preferred_element_type=jnp.float32) * scale  4.37 us
    ppermute x3, waiting for transfers between devices, doubling_sum(): total = total + lax.ppermute(total, name, pairs)  2.41 us
    unnamed x13, local copies, waits for them, and re-layouts  1.87 us
  transfers between devices with their start and end apart: 3, of which 2 were waited for; matrix products, arithmetic and copies ran while one was open for 2% of the time, Pallas kernels for 0%

profile of v1, /device:TPU:0, one launch (start us, length us, event | category | flops | bytes accessed | tf_op | source)
XLA Modules:
  0.0 49.7 jit_solution(6435301905161215542)
XLA Ops:
  0.6 0.0 copy-start
  0.7 0.9 %compare_reduce_fusion = pred[1024]{0:T(1024)(128)(4,1)S(1)} fusion(s32[1024]{0:T(1024)S(1)} %iota_add_fusion, s32[64]{0:T(128)} %param.11), kind=kLoop, calls=%fused_computation.4 | loop fusion | flops 130048 | bytes 5376 | tf_op jit(solution)/shard_map/reduce_or | solution.py:43
  1.6 0.7 %copy-done = bf16[1024,1024]{1,0:T(8,128)(2,1)S(1)} copy-done((bf16[1024,1024]{1,0:T(8,128)(2,1)S(1)}, bf16[1024,1024]{1,0:T(8,128)(2,1)}, u32[]{:S(2)}) %copy-start) | copy-done | bytes 2097176
  2.2 4.4 %select_reduce_fusion = (f32[1024]{0:T(1024)S(1)}, f32[1024]{0:T(1024)S(1)}) fusion(pred[1024]{0:T(1024)(128)(4,1)S(1)} %compare_reduce_fusion, f32[1024]{0:T(1024)} %param.9, f32[1024]{0:T(1024)} %param.8, bf16[1024,1024]{1,0:T(8,128)(2,1)S(1)} %copy-done, bf16[1024,1024]{1,0:T(8,128)(2,1)} %param.10), kind=kOutput, calls=%fused_computation.2 | convolution fusion | flops 2154821632 | bytes 4211712 | tf_op jit(solution)/shard_map/dot_general | solution.py:36
  6.6 0.6 %collective-permute-start = (f32[1024]{0:T(1024)S(1)}, f32[1024]{0:T(1024)S(1)}, u32[]{:S(2)}, u32[]{:S(2)}) collective-permute-start(f32[1024]{0:T(1024)S(1)} %broadcast_multiply_fusion), channel_id=1, source_target_pairs={{0,4},{4,0},{8,12},{12,8},{16,20},{20,16},{24,28},{28,24},{1,5},{5... | collective-permute-start | bytes 12296 | tf_op jit(solution)/shard_map/ppermute | solution.py:13
  7.2 0.8 %collective-permute-done = f32[1024]{0:T(1024)S(1)} collective-permute-done((f32[1024]{0:T(1024)S(1)}, f32[1024]{0:T(1024)S(1)}, u32[]{:S(2)}, u32[]{:S(2)}) %collective-permute-start) | collective-permute-done | bytes 4128 | tf_op jit(solution)/shard_map/ppermute | solution.py:13
  8.0 2.8 %collective-permute-start.1 = (f32[1024]{0:T(1024)S(1)}, f32[1024]{0:T(1024)S(1)}, u32[]{:S(2)}, u32[]{:S(2)}) collective-permute-start(f32[1024]{0:T(1024)S(1)} %fusion), channel_id=1, source_target_pairs={{0,8},{4,12},{8,0},{12,4},{16,24},{20,28},{24,16},{28,20},{1,9},{5... | collective-permute-start | bytes 12296 | tf_op jit(solution)/shard_map/ppermute | solution.py:13
  10.8 1.6 %collective-permute-done.1 = f32[1024]{0:T(1024)S(1)} collective-permute-done((f32[1024]{0:T(1024)S(1)}, f32[1024]{0:T(1024)S(1)}, u32[]{:S(2)}, u32[]{:S(2)}) %collective-permute-start.1) | collective-permute-done | bytes 4128 | tf_op jit(solution)/shard_map/ppermute | solution.py:13
  12.4 2.1 %collective-permute-start.2 = (f32[1024]{0:T(1024)S(1)}, f32[1024]{0:T(1024)S(1)}, u32[]{:S(2)}, u32[]{:S(2)}) collective-permute-start(f32[1024]{0:T(1024)S(1)} %add.53), channel_id=1, source_target_pairs={{0,16},{4,20},{8,24},{12,28},{16,0},{20,4},{24,8},{28,12},{1,17},{... | collective-permute-start | bytes 12296 | tf_op jit(solution)/shard_map/ppermute | solution.py:13
  14.5 11.9 %pmax.7 = f32[1024]{0:T(1024)S(1)} all-reduce(f32[1024]{0:T(1024)S(1)} %get-tuple-element.97), channel_id=1, replica_groups=mesh['pts'=8,'cand'=4] {'cand'}, use_global_device_ids=true, to_apply=%region_7.8 | all-reduce | flops 1024 | bytes 8192 | tf_op jit(solution)/shard_map/pmax | solution.py:45
  26.4 0.6 %max.13 = f32[1024]{0:T(1024)} maximum(f32[1024]{0:T(1024)S(1)} %copy-done.2, f32[1024]{0:T(1024)S(1)} %pmax.7) | non-fusion elementwise | flops 1024 | bytes 12288 | tf_op jit(solution)/shard_map/max | solution.py:46
  27.0 0.6 %dynamic-slice = u32[1]{0:T(128)} dynamic-slice(u32[32]{0:T(128)S(1)} %copy-done.3, u32[]{:T(128)S(6)} %add.57), dynamic_slice_sizes={1} | dynamic-slice | bytes 12
  28.3 4.4 %top_k.14 = (f32[1024]{0:T(1024)S(1)}, s32[1024]{0:T(1024)}) sort(f32[1024]{0:T(1024)S(1)} %add.54, s32[1024]{0:T(1024)S(1)} %iota.11), dimensions={0}, to_apply=%region_1.0 | sort | flops 10240 | bytes 16384 | tf_op jit(solution)/shard_map/top_k | solution.py:41
  32.7 0.1 slice_dynamic-update-slice_fusion
  32.8 8.3 %all-reduce = f32[256]{0:T(256)S(1)} all-reduce(f32[256]{0:T(256)S(1)} %slice_dynamic-update-slice_fusion), channel_id=2, replica_groups=mesh['pts'=8,'cand'=4] {'cand'}, use_global_device_ids=true, to_apply=%add | all-reduce | flops 256 | bytes 2048
  41.1 0.1 reshape.14
  41.2 8.0 %while.15 = (s32[]{:T(128)}, f32[64]{0:T(128)S(1)}, f32[4,64]{1,0:T(4,128)S(1)}, s32[]{:T(128)}, s32[]{:T(128)}, /*index=5*/s32[]{:T(128)}) while((s32[]{:T(128)}, f32[64]{0:T(128)S(1)}, f32[4,64]{1,0:T(4,128)S(1)}, s32[]{:T(128)}, s32[]{:T(128)}, /*index=5*/s32[]{:T(128)}) %tuple.41), condition=%wide.region_4.5_spmd, body=%wide.region_2.4_spmd.sunk | while | flops 1029 | bytes 4211 | solution.py:24
  41.2 0.1 pad_maximum_fusion.2
  41.3 2.6 %top_k.22 = (f32[128]{0:T(128)S(1)}, s32[128]{0:T(128)}) sort(f32[128]{0:T(128)S(1)} %pad_maximum_fusion.2, s32[128]{0:T(128)S(1)} %iota.15), dimensions={0}, to_apply=%region_3.3 | sort | flops 896 | bytes 2048 | tf_op jit(solution)/shard_map/while/body/eval_jaxpr/top_k | solution.py:28
  43.9 0.1 pad_maximum_fusion.2
  44.0 2.6 %top_k.22 = (f32[128]{0:T(128)S(1)}, s32[128]{0:T(128)}) sort(f32[128]{0:T(128)S(1)} %pad_maximum_fusion.2, s32[128]{0:T(128)S(1)} %iota.15), dimensions={0}, to_apply=%region_3.3 | sort | flops 896 | bytes 2048 | tf_op jit(solution)/shard_map/while/body/eval_jaxpr/top_k | solution.py:28
  46.5 0.1 pad_maximum_fusion.2
  46.6 2.6 %top_k.22 = (f32[128]{0:T(128)S(1)}, s32[128]{0:T(128)}) sort(f32[128]{0:T(128)S(1)} %pad_maximum_fusion.2, s32[128]{0:T(128)S(1)} %iota.15), dimensions={0}, to_apply=%region_3.3 | sort | flops 896 | bytes 2048 | tf_op jit(solution)/shard_map/while/body/eval_jaxpr/top_k | solution.py:28
  49.2 0.5 %copy-done.4 = f32[64]{0:T(128)} copy-done((f32[64]{0:T(128)}, f32[64]{0:T(128)S(1)}, u32[]{:S(2)}) %copy-start.4) | copy-done | bytes 280
  (22 shorter events, 0.1 us)
Async XLA Ops:
  0.6 1.6 %copy-start = (bf16[1024,1024]{1,0:T(8,128)(2,1)S(1)}, bf16[1024,1024]{1,0:T(8,128)(2,1)}, u32[]{:S(2)}) copy-start(bf16[1024,1024]{1,0:T(8,128)(2,1)} %param.7) | copy-start | bytes 6291460
  2.2 24.2 %copy-start.2 = (f32[1024]{0:T(1024)S(1)}, f32[1024]{0:T(1024)}, u32[]{:S(2)}) copy-start(f32[1024]{0:T(1024)} %param.9) | copy-start | bytes 12292
  2.2 24.8 %copy-start.3 = (u32[32]{0:T(128)S(1)}, u32[32]{0:T(128)}, u32[]{:S(2)}) copy-start(u32[32]{0:T(128)} %constant.74) | copy-start | bytes 388
  6.6 1.4 %collective-permute-start = (f32[1024]{0:T(1024)S(1)}, f32[1024]{0:T(1024)S(1)}, u32[]{:S(2)}, u32[]{:S(2)}) collective-permute-start(f32[1024]{0:T(1024)S(1)} %broadcast_multiply_fusion), channel_id=1, source_target_pairs={{0,4},{4,0},{8,12},{12,8},{16,20},{20,16},{24,28},{28,24},{1,5},{5... | collective-permute-start | bytes 12296 | tf_op jit(solution)/shard_map/ppermute | solution.py:13
  8.0 4.4 %collective-permute-start.1 = (f32[1024]{0:T(1024)S(1)}, f32[1024]{0:T(1024)S(1)}, u32[]{:S(2)}, u32[]{:S(2)}) collective-permute-start(f32[1024]{0:T(1024)S(1)} %fusion), channel_id=1, source_target_pairs={{0,8},{4,12},{8,0},{12,4},{16,24},{20,28},{24,16},{28,20},{1,9},{5... | collective-permute-start | bytes 12296 | tf_op jit(solution)/shard_map/ppermute | solution.py:13
  12.4 15.8 %collective-permute-start.2 = (f32[1024]{0:T(1024)S(1)}, f32[1024]{0:T(1024)S(1)}, u32[]{:S(2)}, u32[]{:S(2)}) collective-permute-start(f32[1024]{0:T(1024)S(1)} %add.53), channel_id=1, source_target_pairs={{0,16},{4,20},{8,24},{12,28},{16,0},{20,4},{24,8},{28,12},{1,17},{... | collective-permute-start | bytes 12296 | tf_op jit(solution)/shard_map/ppermute | solution.py:13
  28.3 20.9 %copy-start.1 = (f32[1024]{0:T(1024)}, f32[1024]{0:T(1024)S(1)}, u32[]{:S(2)}) copy-start(f32[1024]{0:T(1024)S(1)} %add.54) | copy-start | bytes 12292
  49.2 0.5 %copy-start.4 = (f32[64]{0:T(128)}, f32[64]{0:T(128)S(1)}, u32[]{:S(2)}) copy-start(f32[64]{0:T(128)S(1)} %get-tuple-element.93) | copy-start | bytes 772
